TPU v7x, 128 devices: a whole 4x4x4 slice. The times are simulated.
128 devices in a mesh: expert: 64 (over x, y, z), dp: 2 (over core).
Axes of the slice: x: 4, y: 4, z: 4, core: 2. Of those that a mesh axis runs over, the one named last changes fastest.
Arguments:
- patches: bfloat16 [2048, 196, 1024], P(('dp', 'expert')), parts along dimension 0, may hold values from -6 to 6
- visible: int32 [2048, 49], P(('dp', 'expert')), parts along dimension 0, may hold values from 0 to 195, as said below
- routes: int32 [100352, 1], P(('dp', 'expert')), parts along dimension 0, may hold values from 0 to 63; in each aligned block of 784 rows (0 to 783, 784 to 1567, ...) at most 19 rows name the same one
- expert_cap: int32 [128], P('dp'), parts along dimension 0, may hold values from 8 to 19
- norm_gain: float32 [1024], replicated, may hold values from 0.5 to 2
- norm_bias: float32 [1024], replicated, may hold values from -6 to 6
- router: float32 [1024, 64], replicated, may hold values from -0.1875 to 0.1875
- w_in: bfloat16 [64, 1024, 4096], P('expert'), may hold values from -0.1875 to 0.1875
- b_in: float32 [64, 4096], P('expert'), may hold values from -6 to 6
- w_out: bfloat16 [64, 4096, 1024], P('expert'), may hold values from -0.09375 to 0.09375
- b_out: float32 [64, 1024], P('expert'), may hold values from -6 to 6
Outputs:
- layer_out: bfloat16 [100352, 1024], P(('dp', 'expert')), parts along dimension 0
There are 2 independent parts, one for each index of `dp`. A program takes and returns all parts, laid end to end along the dimension named above; an argument that names none is the same for every part. Nothing has to cross between parts.
Inputs may be any that keep to these rules, and one draw needn't show every extreme that they name: `visible`: each row holds 49 different patch indices in increasing order. `routes`: among the tokens of one index of expert no expert is named more than 19 times.
All inputs are finite; a program needn't handle non-finite values.
Results may differ from a plain program's by a relative error of at most 0.005.
Values may be sent and summed in bfloat16 or wider, within the bound.
A program may use at most 128 MiB of HBM per device.

v0:
```python
import jax
import jax.numpy as jnp
from jax import lax
from jax.sharding import PartitionSpec as P


def items_in_groups(array, axis, split_dim, concat_dim, work, item_dim, out_dim):
    items = jax.tree.leaves(array)[0].shape[item_dim]
    count = 2 if items % 2 == 0 else 1
    done = []
    for k in range(count):
        group = jax.tree.map(
            lambda a: lax.slice_in_dim(
                a, k * (items // count), (k + 1) * (items // count), axis=item_dim
            ),
            array,
        )
        done.append(
            work(
                lax.all_to_all(
                    group, axis, split_axis=split_dim, concat_axis=concat_dim, tiled=True
                )
            )
        )
    return jax.tree.map(lambda *parts: jnp.concatenate(parts, axis=out_dim), *done)


def expert_rows(rows, w_in, b_in, w_out, b_out):
    act = jax.nn.gelu(
        jnp.dot(rows, w_in[0], preferred_element_type=jnp.float32) + b_in[0], approximate=True
    ).astype(jnp.bfloat16)
    return (jnp.dot(act, w_out[0], preferred_element_type=jnp.float32) + b_out[0]).astype(
        jnp.bfloat16
    )


def send_back(result):
    return lax.all_to_all(result, "expert", split_axis=0, concat_axis=0, tiled=True)


def per_device(
    patches, visible, routes, expert_cap, norm_gain, norm_bias, router, w_in, b_in, w_out, b_out
):
    width = patches.shape[2]
    devices = lax.axis_size("expert")
    experts = expert_cap.shape[0]
    x = jnp.take_along_axis(patches, visible[:, :, None], axis=1).reshape(-1, width)
    tok_count = x.shape[0]
    slots = max(2, (3 * tok_count + 2 * experts - 1) // (2 * experts))
    xf = x.astype(jnp.float32)
    mean = jnp.mean(xf, axis=1, keepdims=True)
    var = jnp.mean((xf - mean) ** 2, axis=1, keepdims=True)
    h = (xf - mean) / jnp.sqrt(var + 1e-06) * norm_gain + norm_bias
    hb = h.astype(jnp.bfloat16)
    chosen = routes[:, 0]
    onehot = (chosen[:, None] == jnp.arange(experts, dtype=jnp.int32)[None, :]).astype(jnp.int32)
    logits = jnp.dot(h, router, precision=lax.Precision.HIGHEST)
    gate = jax.nn.sigmoid(jnp.sum(logits * onehot.astype(jnp.float32), axis=1))
    rank = jnp.sum((jnp.cumsum(onehot, axis=0) - onehot) * onehot, axis=1)
    limit = jnp.sum(onehot * expert_cap[None, :], axis=1)
    kept = rank < limit
    dest = jnp.where(kept, chosen * slots + rank, experts * slots)
    outgoing = (
        jnp.zeros((experts * slots + 1, width), jnp.bfloat16)
        .at[dest]
        .set(hb)[:-1]
        .reshape(experts, slots, width)
    )

    def handle(received):
        count = received.shape[1]
        result = expert_rows(received.reshape(-1, width), w_in, b_in, w_out, b_out)
        return send_back(result.reshape(devices, count, width))

    back = items_in_groups(outgoing, "expert", 0, 0, handle, 1, 1)
    flat = back.reshape(experts * slots, width)
    picked = flat[jnp.minimum(dest, experts * slots - 1)].astype(jnp.float32)
    branch = jnp.where(kept[:, None], gate[:, None] * picked, 0.0)
    return (xf + branch).astype(jnp.bfloat16)


def solution(mesh):
    return jax.shard_map(
        per_device,
        mesh=mesh,
        in_specs=(
            P(("dp", "expert"), None, None),
            P(("dp", "expert"), None),
            P(("dp", "expert"), None),
            P("dp"),
            P(),
            P(),
            P(),
            P("expert", None, None),
            P("expert", None),
            P("expert", None, None),
            P("expert", None),
        ),
        out_specs=P(("dp", "expert"), None),
        check_vma=False,
    )
```

profile of v0, /device:TPU:0, one launch (start us, length us, event | category | flops | bytes accessed | tf_op | source)
XLA Modules:
  0.0 189.9 jit_solution(10765539927735940309)
XLA Ops:
  0.0 0.0 copy-start
  0.0 0.7 compare_and_fusion
  0.8 0.7 bitcast_or_fusion
  1.5 0.1 broadcast_in_dim.44
  1.5 0.1 reshape.116
  1.6 14.9 %gather_fusion.1 = bf16[784,1024]{1,0:T(8,128)(2,1)S(1)} fusion(bf16[16,196,1024]{2,0,1:T(8,128)(2,1)} %param.11, s32[784]{0:T(1024)S(1)} %reshape.116), kind=kCustom, calls=%fused_computation.1 | custom fusion | bytes 3217536 | tf_op jit(solution)/shard_map/jit(take_along_axis)/gather | solution.py:47
  16.6 0.0 copy-start.1
  16.6 0.0 copy-start.2
  16.6 1.8 reshape.119
  18.3 0.0 copy-start.5
  18.3 0.0 copy-start.3
  18.4 0.0 copy-start.4
  18.4 2.1 %convert_reduce_fusion = f32[16,49]{1,0:T(8,128)S(1)} fusion(bf16[16,49,1024]{2,1,0:T(8,128)(2,1)} %reshape.119, pred[16,49]{1,0:T(8,128)(4,1)S(1)} %compare_and_fusion), kind=kLoop, calls=%fused_computation.22 | loop fusion | flops 2407664 | bytes 1609552 | tf_op jit(solution)/shard_map/reduce_sum | solution.py:51
  20.4 2.3 %fusion.22 = f32[16,49]{1,0:T(8,128)S(1)} fusion(f32[16,49]{1,0:T(8,128)S(1)} %broadcast_multiply_fusion, bf16[16,49,1024]{2,1,0:T(8,128)(2,1)} %reshape.119, pred[16,49]{1,0:T(8,128)(4,1)S(1)} %compare_and_fusion), kind=kLoop, calls=%fused_computation.26 | loop fusion | flops 4013296 | bytes 1612688 | tf_op jit(solution)/shard_map/reduce_sum | solution.py:52
  22.8 0.1 div.24
  22.9 0.0 copy-done.2
  23.0 2.1 %reduce-window.6 = s32[64,7,128]{2,0,1:T(8,128)S(1)} reduce-window(s32[64,7,128]{2,0,1:T(8,128)S(1)} %copy_bitcast_fusion, s32[]{:T(128)} %constant.17.clone.1), window={size=1x1x128 pad=0_0x0_0x127_0}, to_apply=%region_0.0 | reduce-window | flops 7282688 | bytes 458756 | tf_op jit(solution)/shard_map/reduce-window
  25.1 0.3 slice_reduce_fusion
  25.4 0.1 bitcast_bitcast_fusion
  25.6 0.1 sqrt.12
  25.6 0.0 copy-done.5
  25.7 0.1 fusion.32
  25.8 0.0 copy-done.3
  25.8 0.0 copy-done.4
  25.8 8.6 %scatter_custom_fusion = bf16[1217,1024]{1,0:T(8,128)(2,1)} fusion(s32[784]{0:T(1024)S(1)} %get-tuple-element.8, bf16[]{:T(256)} %constant.26.clone.1, f32[1024]{0:T(1024)S(1)} %copy-done.3, f32[1024]{0:T(1024)S(1)} %copy-done.4, f32[784]{0:T(1024)S(1)} %sqrt.12, f32[784]{0:T(1024)S(1)} %div.24, bf16[784,1024]{1,0:T(8,128)(2,1)S(1)} %gather_fusion.1, ...), kind=kCustom, calls=%fused_computation.32 | custom fusion | flops 5619712 | bytes 4115458 | tf_op jit(solution)/shard_map/scatter | solution.py:66
  34.4 3.4 %slice.22 = bf16[1216,1024]{1,0:T(8,128)(2,1)} slice(bf16[1217,1024]{1,0:T(8,128)(2,1)} %scatter_custom_fusion), slice={[0:1216], [0:1024]} | slice | bytes 4980736 | tf_op jit(solution)/shard_map/slice | solution.py:64
  37.8 4.4 %reshape.103 = bf16[64,19,1024]{2,1,0:T(8,128)(2,1)} reshape(bf16[1216,1024]{1,0:T(8,128)(2,1)} %slice.22) | data formatting | bytes 4980736 | tf_op jit(solution)/shard_map/reshape | solution.py:67
  42.2 52.7 %all_to_all.10 = bf16[64,19,1024]{2,1,0:T(8,128)(2,1)} all-to-all(bf16[64,19,1024]{2,1,0:T(8,128)(2,1)} %reshape.103), channel_id=1, replica_groups=mesh['expert'=64,'dp'=2] {'expert'}, dimensions={0} | all-to-all | bytes 4980736 | tf_op jit(solution)/shard_map/all_to_all | solution.py:20
  94.9 0.0 copy-start.6
  94.9 0.0 copy-start.7
  94.9 4.4 %reshape.104 = bf16[1216,1024]{1,0:T(8,128)(2,1)} reshape(bf16[64,19,1024]{2,1,0:T(8,128)(2,1)} %all_to_all.10) | data formatting | bytes 4980736 | tf_op jit(solution)/shard_map/reshape | solution.py:72
  99.4 0.0 copy-done.6
  99.4 0.0 copy-done.7
  99.4 31.0 %add_convert_fusion = bf16[1216,1024]{1,0:T(8,128)(2,1)} fusion(bf16[1,4096,1024]{2,1,0:T(8,128)(2,1)} %param.20, bf16[1216,1024]{1,0:T(8,128)(2,1)} %reshape.104, f32[4096]{0:T(1024)S(1)} %bitcast.34, bf16[1,1024,4096]{2,1,0:T(8,128)(2,1)} %param.18, f32[1024]{0:T(1024)S(1)} %bitcast.35), kind=kOutput, calls=%fused_computation.20 | convolution fusion | flops 20453392384 | bytes 21778432 | tf_op jit(solution)/shard_map/dot_general | solution.py:32
  130.4 4.4 %reshape.105 = bf16[64,19,1024]{2,1,0:T(8,128)(2,1)} reshape(bf16[1216,1024]{1,0:T(8,128)(2,1)} %add_convert_fusion) | data formatting | bytes 4980736 | tf_op jit(solution)/shard_map/reshape | solution.py:73
  134.8 5.6 %all-to-all-start.1 = ((bf16[64,19,1024]{2,1,0:T(8,128)(2,1)}), bf16[64,19,1024]{2,1,0:T(8,128)(2,1)}, u32[]{:S(2)}, u32[]{:S(2)}) async-start(bf16[64,19,1024]{2,1,0:T(8,128)(2,1)} %reshape.105), calls=%async_computation.1 | async-start | bytes 6291456 | tf_op jit(solution)/shard_map/all_to_all | solution.py:38
  140.4 0.0 copy-done.1
  140.4 0.0 copy-done
  140.4 3.8 %fusion.30 = f32[784]{0:T(1024)S(1)} fusion(f32[1024,64]{0,1:T(8,128)S(1)} %copy-done, s32[784]{0:T(1024)S(1)} %reduce.2, f32[1024]{0:T(1024)S(1)} %copy-done.3, f32[1024]{0:T(1024)S(1)} %copy-done.4, f32[784]{0:T(1024)S(1)} %sqrt.12, f32[784]{0:T(1024)S(1)} %div.24, bf16[784,1024]{1,0:T(8,128)(2,1)S(1)} %gather_fusion.1, ...), kind=kOutput, calls=%fused_computation.37 | convolution fusion | flops 621629696 | bytes 1889296 | tf_op jit(solution)/shard_map/dot_general | solution.py:57
  144.2 35.4 %all-to-all-done.1 = bf16[64,19,1024]{2,1,0:T(8,128)(2,1)} async-done(((bf16[64,19,1024]{2,1,0:T(8,128)(2,1)}), bf16[64,19,1024]{2,1,0:T(8,128)(2,1)}, u32[]{:S(2)}, u32[]{:S(2)}) %all-to-all-start.1) | async-done | bytes 2490400 | tf_op jit(solution)/shard_map/all_to_all | solution.py:38
  179.6 3.0 %reshape.106 = bf16[1216,1024]{1,0:T(8,128)(2,1)S(1)} reshape(bf16[64,19,1024]{2,1,0:T(8,128)(2,1)} %all-to-all-done.1) | data formatting | bytes 4980736 | tf_op jit(solution)/shard_map/reshape | solution.py:76
  182.6 4.1 %gather_fusion = bf16[784,1024]{1,0:T(8,128)(2,1)} fusion(bf16[1216,1024]{1,0:T(8,128)(2,1)S(1)} %reshape.106, s32[1024]{0:T(1024)S(1)} %pad_clamp_fusion), kind=kCustom, calls=%fused_computation | custom fusion | bytes 3214400 | tf_op jit(solution)/shard_map/gather | solution.py:77
  186.7 3.2 %fusion.26 = bf16[784,1024]{1,0:T(8,128)(2,1)} fusion(bf16[784,1024]{1,0:T(8,128)(2,1)} %gather_fusion, f32[784]{0:T(1024)S(1)} %add_divide_fusion, pred[784]{0:T(1024)(128)(4,1)S(1)} %lt.29, bf16[784,1024]{1,0:T(8,128)(2,1)} %copy-done.1, pred[784]{0:T(1024)(128)(4,1)S(1)} %broadcast_in_dim.44), kind=kLoop, calls=%fused_computation.30 | loop fusion | flops 5619712 | bytes 4821600 | tf_op jit(solution)/shard_map/convert_element_type | solution.py:79
  (10 shorter events, 0.2 us)
Async XLA Ops:
  0.0 140.4 %copy-start = (f32[1024,64]{0,1:T(8,128)S(1)}, f32[1024,64]{0,1:T(8,128)}, u32[]{:S(2)}) copy-start(f32[1024,64]{0,1:T(8,128)} %param.17) | copy-start | bytes 786436
  16.6 123.8 %copy-start.1 = (bf16[784,1024]{1,0:T(8,128)(2,1)}, bf16[784,1024]{1,0:T(8,128)(2,1)S(1)}, u32[]{:S(2)}) copy-start(bf16[784,1024]{1,0:T(8,128)(2,1)S(1)} %gather_fusion.1) | copy-start | bytes 4816900
  16.6 6.3 %copy-start.2 = (s32[784,1]{0,1:T(1,128)S(1)}, s32[784,1]{0,1:T(1,128)}, u32[]{:S(2)}) copy-start(s32[784,1]{0,1:T(1,128)} %param.13) | copy-start | bytes 9412
  18.3 7.3 %copy-start.5 = (s32[64]{0:T(128)S(1)}, s32[64]{0:T(128)}, u32[]{:S(2)}) copy-start(s32[64]{0:T(128)} %param.14) | copy-start | bytes 772
  18.3 7.5 %copy-start.3 = (f32[1024]{0:T(1024)S(1)}, f32[1024]{0:T(1024)}, u32[]{:S(2)}) copy-start(f32[1024]{0:T(1024)} %param.16) | copy-start | bytes 12292
  18.4 7.5 %copy-start.4 = (f32[1024]{0:T(1024)S(1)}, f32[1024]{0:T(1024)}, u32[]{:S(2)}) copy-start(f32[1024]{0:T(1024)} %param.15) | copy-start | bytes 12292
  94.9 4.5 %copy-start.6 = (f32[1,4096]{1,0:T(1,128)S(1)}, f32[1,4096]{1,0:T(1,128)}, u32[]{:S(2)}) copy-start(f32[1,4096]{1,0:T(1,128)} %param.19) | copy-start | bytes 49156
  94.9 4.5 %copy-start.7 = (f32[1,1024]{1,0:T(1,128)S(1)}, f32[1,1024]{1,0:T(1,128)}, u32[]{:S(2)}) copy-start(f32[1,1024]{1,0:T(1,128)} %param.21) | copy-start | bytes 12292
  134.8 44.8 %all-to-all-start.1 = ((bf16[64,19,1024]{2,1,0:T(8,128)(2,1)}), bf16[64,19,1024]{2,1,0:T(8,128)(2,1)}, u32[]{:S(2)}, u32[]{:S(2)}) async-start(bf16[64,19,1024]{2,1,0:T(8,128)(2,1)} %reshape.105), calls=%async_computation.1 | async-start | bytes 6291456 | tf_op jit(solution)/shard_map/all_to_all | solution.py:38
where the time goes:
time: 191 us; the launch traced here: 190 us
  blocking collectives  52.7 us (28%)
  local copies, waits for them, and re-layouts  41.1 us (22%)
  waiting for transfers between devices  35.4 us (19%)
  matrix products  34.8 us (18%)
  other arithmetic  20.1 us (11%)
  starting transfers between devices  5.58 us (3%)
    all_to_all x1, blocking collectives, items_in_groups(): lax.all_to_all(group, axis, split_axis=split_dim, concat_axis=concat_dim,...  52.7 us
    all_to_all x1, waiting for transfers between devices, send_back(): lax.all_to_all(result, 'expert', split_axis=0, concat_axis=0, tiled=True)  35.4 us
    dot_general x1, matrix products, expert_rows(): jnp.dot(act, w_out[0], preferred_element_type=jnp.float32) + b_out[0]  31 us
    gather x3, local copies, waits for them, and re-layouts, per_device(): jnp.take_along_axis(patches, visible[:, :, None], axis=1).reshape(-1, width)  16.8 us
    scatter x1, other arithmetic, per_device(): outgoing = jnp.zeros((experts * slots + 1, width), jnp.bfloat16).at[dest]...  8.6 us
    all_to_all x1, starting transfers between devices, send_back(): lax.all_to_all(result, 'expert', split_axis=0, concat_axis=0, tiled=True)  5.58 us
    reshape x1, local copies, waits for them, and re-layouts, handle(): result = expert_rows(received.reshape(-1, width), w_in, b_in, w_out, b_out)  4.44 us
    reshape x1, local copies, waits for them, and re-layouts, per_device(): outgoing = jnp.zeros((experts * slots + 1, width), jnp.bfloat16).at[dest]...  4.39 us
  transfers between devices with their start and end apart: 1, of which 1 were waited for; matrix products, arithmetic and copies ran while one was open for 2% of the time, Pallas kernels for 0%

commit v1 on v0

v1 whole, which is shorter than its diff:
```python
import itertools

import jax
import jax.numpy as jnp
from jax import lax
from jax.experimental import pallas as pl
from jax.experimental.pallas import tpu as pltpu
from jax.sharding import PartitionSpec as P

MESH = pl.DeviceIdType.MESH
SIDE = 4
LANES = 128
PLACES = sorted(
    itertools.product(range(SIDE), repeat=3), key=lambda o: (sum(min(d, SIDE - d) for d in o) > 0, (o[0] * 7 + o[1] * 11 + o[2] * 13) % 16)
)
CHUNK = 16


def prep_kernel(
    patches, visible, route_row, route_col, cap_row, cap_col, gain, bias, router,
    blocks, x_out, gate_out, key_out, hb_ref, h_lo, tail,
):
    images, width = patches.shape[1], patches.shape[2]
    keep = visible.shape[1]
    toks = images * keep
    experts = cap_col.shape[0]

    row = lax.broadcasted_iota(jnp.int32, (images, width), 0)

    def pick(k, carry):
        got = patches[visible[0, k]]
        for i in range(1, images):
            got = jnp.where(row == i, patches[visible[i, k]], got)
        start = pl.multiple_of(k * images, images)
        x_out[pl.ds(start, images), :] = got
        xf = got.astype(jnp.float32)
        mean = jnp.sum(xf, axis=1, keepdims=True) * (1.0 / width)
        diff = xf - mean
        var = jnp.sum(diff * diff, axis=1, keepdims=True) * (1.0 / width)
        h = diff * (1.0 / jnp.sqrt(var + 1e-06)) * gain[...] + bias[...]
        hb = h.astype(jnp.bfloat16)
        hb_ref[pl.ds(start, images), :] = hb
        h_lo[pl.ds(start, images), :] = (h - hb.astype(jnp.float32)).astype(jnp.bfloat16)
        return carry

    lax.fori_loop(0, keep, pick, 0)

    def place(shape, dim):
        t = lax.broadcasted_iota(jnp.int32, shape, dim)
        return (t % images) * keep + t // images

    earlier = (place((toks, 1), 0) < place((1, toks), 1)).astype(jnp.bfloat16)
    later = (place((toks, 1), 0) > place((1, toks), 1)).astype(jnp.bfloat16)
    one_row = lax.broadcasted_iota(jnp.int32, (experts, toks), 0) == route_row[...]
    ones = one_row.astype(jnp.float32)
    before = jnp.dot(ones.astype(jnp.bfloat16), earlier, preferred_element_type=jnp.float32)
    rank = jnp.sum(before * ones, axis=0, keepdims=True).astype(jnp.int32)
    limit = jnp.sum(jnp.where(one_row, cap_col[...], 0), axis=0, keepdims=True)
    kept = rank < limit
    chosen = route_row[...]

    hb = hb_ref[...]

    def rows_of(key, count):
        sel = lax.broadcasted_iota(jnp.int32, (count, toks), 0) == key
        return jnp.dot(sel.astype(jnp.bfloat16), hb, preferred_element_type=jnp.float32)

    for part in range(2):
        key = jnp.where(kept & (rank // 8 == part), chosen * 8 + rank % 8, -1)
        got = rows_of(key, experts * 8)
        blocks[:, :, part * width : (part + 1) * width] = got.reshape(experts, 8, width).astype(
            jnp.bfloat16
        )
    key = jnp.where(kept & (rank >= 16), (rank - 16) * experts + chosen, -1)
    got = rows_of(key, experts * 3)
    for r in range(3):
        for j in range(8):
            tail[r, pl.ds(j, experts, stride=8), :] = got[
                r * experts : (r + 1) * experts, j * LANES : (j + 1) * LANES
            ]
        blocks[:, :, 2 * width + r * LANES : 2 * width + (r + 1) * LANES] = (
            tail[r].reshape(experts, 8, LANES).astype(jnp.bfloat16)
        )

    one_col = lax.broadcasted_iota(jnp.int32, (toks, experts), 1) == route_col[...]
    ones_c = one_col.astype(jnp.float32)
    before_c = jnp.dot(later, ones_c.astype(jnp.bfloat16), preferred_element_type=jnp.float32)
    rank_c = jnp.sum(before_c * ones_c, axis=1, keepdims=True).astype(jnp.int32)
    limit_c = jnp.sum(jnp.where(one_col, cap_row[...], 0), axis=1, keepdims=True)
    chosen_c = route_col[...]
    slot = jnp.where(
        rank_c < 8,
        chosen_c * 8 + rank_c,
        jnp.where(
            rank_c < 16,
            experts * 8 + chosen_c * 8 + rank_c - 8,
            experts * rank_c + chosen_c,
        ),
    )
    key_out[...] = jnp.where(rank_c < limit_c, slot, -1)
    r_full = router[...]
    r_hi = r_full.astype(jnp.bfloat16)
    r_lo = (r_full - r_hi.astype(jnp.float32)).astype(jnp.bfloat16)
    logits = (
        jnp.dot(hb, r_lo, preferred_element_type=jnp.float32)
        + jnp.dot(h_lo[...], r_hi, preferred_element_type=jnp.float32)
        + jnp.dot(hb, r_hi, preferred_element_type=jnp.float32)
    )
    score = jnp.sum(logits * ones_c, axis=1, keepdims=True)
    gate_out[...] = 1.0 / (1.0 + jnp.exp(-score))


def exchange_kernel(
    blocks, w_in, b_in, w_out, b_out, back,
    sent, got, made, w1, w2, rows, act, tail, rest,
    load_sem, s_sem, r_sem, ys_sem, yr_sem,
):
    width, hidden = w1.shape
    me = lax.axis_index("expert")
    mx, my, mz = me // (SIDE * SIDE), (me // SIDE) % SIDE, me % SIDE

    def at(o, sign):
        x = (mx + sign * o[0] + SIDE) % SIDE
        y = (my + sign * o[1] + SIDE) % SIDE
        z = (mz + sign * o[2] + SIDE) % SIDE
        return (x * SIDE + y) * SIDE + z

    load = pltpu.make_async_copy(blocks, sent, load_sem.at[0])
    load.start()
    load1 = pltpu.make_async_copy(w_in.at[0], w1, load_sem.at[1])
    load1.start()
    load2 = pltpu.make_async_copy(w_out.at[0], w2, load_sem.at[2])
    load2.start()

    barrier = pltpu.get_barrier_semaphore()
    for o in PLACES[1:]:
        pl.semaphore_signal(barrier, inc=1, device_id={"expert": at(o, 1)}, device_id_type=MESH)
    pl.semaphore_wait(barrier, len(PLACES) - 1)
    load.wait()

    def out_copy(i):
        peer = at(PLACES[i], 1)
        return pltpu.make_async_remote_copy(
            src_ref=sent.at[peer], dst_ref=got.at[i], send_sem=s_sem.at[i], recv_sem=r_sem.at[i],
            device_id={"expert": peer}, device_id_type=MESH,
        )

    def back_copy(i):
        peer = at(PLACES[i], -1)
        return pltpu.make_async_remote_copy(
            src_ref=made.at[i], dst_ref=back.at[me], send_sem=ys_sem.at[i], recv_sem=yr_sem.at[i],
            device_id={"expert": peer}, device_id_type=MESH,
        )

    count = len(PLACES)
    for i in range(1, count):
        out_copy(i).start()
    got[0] = sent[me]
    step = 512
    wide = 256
    for c in range(count // CHUNK):
        lo = c * CHUNK
        for i in range(max(lo, 1), lo + CHUNK):
            out_copy(i).wait_recv()
        half = CHUNK * 8
        for part in range(2):
            piece = got[lo : lo + CHUNK, :, part * width : (part + 1) * width]
            rows[part * half : (part + 1) * half, :] = (
                piece.astype(jnp.float32).reshape(half, width).astype(jnp.bfloat16)
            )
        for r in range(3):
            tail[r] = (
                got[lo : lo + CHUNK, :, 2 * width + r * LANES : 2 * width + (r + 1) * LANES]
                .astype(jnp.float32)
                .reshape(half, LANES)
            )
            for j in range(8):
                at_row = 2 * half + r * CHUNK
                rows[at_row : at_row + CHUNK, j * LANES : (j + 1) * LANES] = tail[
                    r, pl.ds(j, CHUNK, stride=8), :
                ].astype(jnp.bfloat16)
        if c == 0:
            load1.wait()
            load2.wait()

        @pl.loop(0, hidden // step)
        def _(f):
            cols = pl.ds(pl.multiple_of(f * step, step), step)
            v = jnp.dot(rows[...], w1[:, cols], preferred_element_type=jnp.float32) + b_in[:, cols]
            inner = v * (0.7978845608028654 + 0.035677408136300125 * (v * v))
            half_v = 0.5 * v
            act[:, cols] = (half_v + half_v * jnp.tanh(inner)).astype(jnp.bfloat16)

        @pl.loop(0, width // wide)
        def _(n):
            cols = pl.ds(pl.multiple_of(n * wide, wide), wide)
            y = jnp.dot(act[...], w2[:, cols], preferred_element_type=jnp.float32) + b_out[:, cols]
            for part in range(2):
                made[lo : lo + CHUNK, :, pl.ds(pl.multiple_of(part * width + n * wide, wide), wide)] = (
                    y[part * half : (part + 1) * half].reshape(CHUNK, 8, wide).astype(jnp.bfloat16)
                )
            rest[:, cols] = y[2 * half :]

        for r in range(3):
            for j in range(8):
                tail[r, pl.ds(j, CHUNK, stride=8), :] = rest[
                    r * CHUNK : (r + 1) * CHUNK, j * LANES : (j + 1) * LANES
                ]
            made[lo : lo + CHUNK, :, 2 * width + r * LANES : 2 * width + (r + 1) * LANES] = (
                tail[r].reshape(CHUNK, 8, LANES).astype(jnp.bfloat16)
            )
        for i in range(max(lo, 1), lo + CHUNK):
            back_copy(i).start()
        if c == 0:
            own = pltpu.make_async_copy(made.at[0], back.at[me], load_sem.at[3])
            own.start()
    own.wait()
    for i in range(1, count):
        out_copy(i).wait_send()
        back_copy(i).wait_send()
    for i in range(1, count):
        back_copy(i).wait_recv()


def combine_kernel(back, x_ref, gate, key, out, sel, rest, tail, perm, joined):
    experts = back.shape[0]
    toks, width = x_ref.shape
    slots = sel.shape[1]
    images, keep = 16, toks // 16
    sel[...] = (lax.broadcasted_iota(jnp.int32, (toks, slots), 1) == key[...]).astype(jnp.bfloat16)
    t_row = lax.broadcasted_iota(jnp.int32, (1, toks), 1)
    place = (t_row % images) * keep + t_row // images
    perm[...] = (lax.broadcasted_iota(jnp.int32, (toks, toks), 0) == place).astype(jnp.bfloat16)
    for r in range(3):
        tail[r] = (
            back[:, :, 2 * width + r * LANES : 2 * width + (r + 1) * LANES]
            .astype(jnp.float32)
            .reshape(experts * 8, LANES)
        )
        for j in range(8):
            rest[r * experts : (r + 1) * experts, j * LANES : (j + 1) * LANES] = tail[
                r, pl.ds(j, experts, stride=8), :
            ].astype(jnp.bfloat16)
    wide = 256
    for n in range(width // wide):
        cols = slice(n * wide, (n + 1) * wide)
        for part in range(2):
            piece = back[:, :, part * width + n * wide : part * width + (n + 1) * wide]
            joined[part * experts * 8 : (part + 1) * experts * 8, :] = (
                piece.astype(jnp.float32).reshape(experts * 8, wide).astype(jnp.bfloat16)
            )
        joined[2 * experts * 8 :, :] = rest[:, cols]
        f = jnp.dot(sel[...], joined[...], preferred_element_type=jnp.float32)
        total = (x_ref[:, cols].astype(jnp.float32) + gate[...] * f).astype(jnp.bfloat16)
        out[:, cols] = jnp.dot(perm[...], total, preferred_element_type=jnp.float32).astype(
            jnp.bfloat16
        )


def per_device(
    patches, visible, routes, expert_cap, norm_gain, norm_bias, router, w_in, b_in, w_out, b_out
):
    images, _, width = patches.shape
    keep = visible.shape[1]
    toks = images * keep
    experts = expert_cap.shape[0]
    hidden = w_in.shape[2]
    by_patch = jnp.transpose(patches, (1, 0, 2))
    route = routes.reshape(images, keep).T.reshape(1, toks)
    vmem = pl.BlockSpec(memory_space=pltpu.VMEM)
    smem = pl.BlockSpec(memory_space=pltpu.SMEM)
    any_ = pl.BlockSpec(memory_space=pl.ANY)
    blk = (experts, 8, 2 * width + 3 * LANES)
    half = CHUNK * 8
    sent, x, gate, key = pl.pallas_call(
        prep_kernel,
        out_shape=(
            jax.ShapeDtypeStruct(blk, jnp.bfloat16),
            jax.ShapeDtypeStruct((toks, width), jnp.bfloat16),
            jax.ShapeDtypeStruct((toks, 1), jnp.float32),
            jax.ShapeDtypeStruct((toks, 1), jnp.int32),
        ),
        in_specs=[vmem, smem] + [vmem] * 7,
        out_specs=(vmem,) * 4,
        scratch_shapes=[
            pltpu.VMEM((toks, width), jnp.bfloat16),
            pltpu.VMEM((toks, width), jnp.bfloat16),
            pltpu.VMEM((3, experts * 8, LANES), jnp.float32),
        ],
        compiler_params=pltpu.CompilerParams(vmem_limit_bytes=56 * 2**20),
        name="prep",
    )(
        by_patch, visible, route, route.reshape(toks, 1), expert_cap.reshape(1, experts),
        expert_cap.reshape(experts, 1), norm_gain.reshape(1, width), norm_bias.reshape(1, width), router,
    )
    back = pl.pallas_call(
        exchange_kernel,
        out_shape=jax.ShapeDtypeStruct(blk, jnp.bfloat16),
        in_specs=[any_, any_, vmem, any_, vmem],
        out_specs=any_,
        scratch_shapes=[
            pltpu.VMEM(blk, jnp.bfloat16),
            pltpu.VMEM(blk, jnp.bfloat16),
            pltpu.VMEM(blk, jnp.bfloat16),
            pltpu.VMEM((width, hidden), jnp.bfloat16),
            pltpu.VMEM((hidden, width), jnp.bfloat16),
            pltpu.VMEM((CHUNK * 19, width), jnp.bfloat16),
            pltpu.VMEM((CHUNK * 19, hidden), jnp.bfloat16),
            pltpu.VMEM((3, half, LANES), jnp.float32),
            pltpu.VMEM((CHUNK * 3, width), jnp.float32),
            pltpu.SemaphoreType.DMA((4,)),
            pltpu.SemaphoreType.DMA((experts,)),
            pltpu.SemaphoreType.DMA((experts,)),
            pltpu.SemaphoreType.DMA((experts,)),
            pltpu.SemaphoreType.DMA((experts,)),
        ],
        compiler_params=pltpu.CompilerParams(
            collective_id=0, has_side_effects=True, vmem_limit_bytes=56 * 2**20
        ),
        name="exchange",
    )(sent, w_in, b_in, w_out, b_out)
    return pl.pallas_call(
        combine_kernel,
        out_shape=jax.ShapeDtypeStruct((toks, width), jnp.bfloat16),
        in_specs=[vmem] * 4,
        out_specs=vmem,
        scratch_shapes=[
            pltpu.VMEM((toks, experts * 19), jnp.bfloat16),
            pltpu.VMEM((experts * 3, width), jnp.bfloat16),
            pltpu.VMEM((3, experts * 8, LANES), jnp.float32),
            pltpu.VMEM((toks, toks), jnp.bfloat16),
            pltpu.VMEM((experts * 19, 256), jnp.bfloat16),
        ],
        compiler_params=pltpu.CompilerParams(vmem_limit_bytes=56 * 2**20),
        name="combine",
    )(back, x, gate, key)


def solution(mesh):
    return jax.shard_map(
        per_device,
        mesh=mesh,
        in_specs=(
            P(("dp", "expert"), None, None),
            P(("dp", "expert"), None),
            P(("dp", "expert"), None),
            P("dp"),
            P(),
            P(),
            P(),
            P("expert", None, None),
            P("expert", None),
            P("expert", None, None),
            P("expert", None),
        ),
        out_specs=P(("dp", "expert"), None),
        check_vma=False,
    )
```

time: 191 us -> 109 us (0.57)
  Pallas kernels: 0 us -> 102 us
  blocking collectives: 52.7 us -> 0 us
  local copies, waits for them, and re-layouts: 41.1 us -> 5.15 us
  waiting for transfers between devices: 35.4 us -> 0 us
  matrix products: 34.8 us -> 0 us
  other arithmetic: 20.1 us -> 0.7 us
  starting transfers between devices: 5.58 us -> 0 us
    pallas_call x0 -> x3, Pallas kernels: none -> 102 us  [the longest x1 70.2 us: per_device(): pl.pallas_call(exchange_kernel, out_shape=jax.ShapeDtypeStruct(blk, jnp.b...]
    all_to_all x1 -> x0, blocking collectives: 52.7 us -> none  [items_in_groups(): lax.all_to_all(group, axis, split_axis=split_dim, concat_axis=concat_dim,...]
    all_to_all x1 -> x0, waiting for transfers between devices: 35.4 us -> none  [send_back(): lax.all_to_all(result, 'expert', split_axis=0, concat_axis=0, tiled=True)]
    dot_general x2 -> x0, matrix products: 34.8 us -> none  [the longest x1 31 us: expert_rows(): jnp.dot(act, w_out[0], preferred_element_type=jnp.float32) + b_out[0]]
    gather x4 -> x0, local copies, waits for them, and re-layouts: 20.9 us -> none  [the longest x3 16.8 us: per_device(): jnp.take_along_axis(patches, visible[:, :, None], axis=1).reshape(-1, width)]
    reshape x4, local copies, waits for them, and re-layouts: 16.2 us -> 2.19 us  [the longest x1 1.35 us: per_device(): expert_cap.reshape(experts, 1)]
    scatter x1 -> x0, other arithmetic: 8.6 us -> none  [per_device(): outgoing = jnp.zeros((experts * slots + 1, width), jnp.bfloat16).at[dest]...]
    all_to_all x1 -> x0, starting transfers between devices: 5.58 us -> none  [send_back(): lax.all_to_all(result, 'expert', split_axis=0, concat_axis=0, tiled=True)]
  transfers between devices with their start and end apart: 1 -> 0, of which waited for: 1 -> 0; matrix products, arithmetic and copies ran while one was open for 2% -> 0% of each run, Pallas kernels for 0% -> 0%
where the time goes in v1:
time: 109 us; the launch traced here: 108 us
  Pallas kernels  102 us (94%)
  local copies, waits for them, and re-layouts  5.15 us (5%)
    pallas_call x1, Pallas kernels, per_device(): pl.pallas_call(exchange_kernel, out_shape=jax.ShapeDtypeStruct(blk, jnp.b...  70.2 us
    pallas_call x1, Pallas kernels, per_device(): pl.pallas_call(prep_kernel, out_shape=(jax.ShapeDtypeStruct(blk, jnp.bflo...  20.1 us
    pallas_call x1, Pallas kernels, per_device(): pl.pallas_call(combine_kernel, out_shape=jax.ShapeDtypeStruct((toks, widt...  11.4 us

profile of v1, /device:TPU:0, one launch (start us, length us, event | category | flops | bytes accessed | tf_op | source)
XLA Modules:
  0.0 107.5 jit_solution(9767708785604907740)
XLA Ops:
  0.0 0.7 reduce
  0.7 0.1 reshape.18
  0.8 0.1 copy.15
  0.9 0.7 reshape.19.route_row
  1.5 1.4 %copy.17.cap_col = s32[64,1]{1,0:T(8,128)} copy(s32[64,1]{0,1:T(1,128)} %bitcast.11) | data formatting | bytes 512 | tf_op jit(solution)/shard_map/reshape | solution.py:294
  2.9 1.0 reshape_reshape.4.route_col
  3.9 1.9 %copy.18.router = f32[1024,64]{1,0:T(8,128)} copy(f32[1024,64]{0,1:T(8,128)} %param.17) | data formatting | bytes 524288 | tf_op args[6]
  5.9 20.1 %prep.1 = (bf16[64,8,2432]{2,1,0:T(8,128)(2,1)}, bf16[784,1024]{1,0:T(8,128)(2,1)}, f32[784,1]{1,0:T(8,128)}, s32[784,1]{1,0:T(8,128)}) custom-call(bf16[196,16,1024]{2,1,0:T(8,128)(2,1)} %bitcast.6, s32[16,49]{1,0:T(8,128)} %visible.1, s32[1,784]{1,0:T(1,128)} %reshape.19.route_row, s32[784,1]{1,0:T(8,128)} %reshape_reshape.4.route_col, s32[1,64]{1,0:T(1,128)} %bitcast.12, ...), custom_call_target="tpu_custom_call" | custom-call | tf_op jit(solution)/shard_map/prep/pallas_call | solution.py:275
  25.9 70.2 %exchange.1.back = bf16[64,8,2432]{2,1,0:T(8,128)(2,1)} custom-call(bf16[64,8,2432]{2,1,0:T(8,128)(2,1)} %get-tuple-element.9.blocks, bf16[1,1024,4096]{2,1,0:T(8,128)(2,1)} %w_in.1, f32[1,4096]{1,0:T(1,128)} %b_in.1, bf16[1,4096,1024]{2,1,0:T(8,128)(2,1)} %w_out.1, f32[1,1024]{1,0:T(1,128)} %b_out.1), custom_call_target="tpu_custom_call" | custom-call | tf_op jit(solution)/shard_map/exchange/pallas_call | solution.py:296
  96.1 11.4 %combine.1 = bf16[784,1024]{1,0:T(8,128)(2,1)} custom-call(bf16[64,8,2432]{2,1,0:T(8,128)(2,1)} %exchange.1.back, bf16[784,1024]{1,0:T(8,128)(2,1)} %get-tuple-element.10.x_ref, f32[784,1]{1,0:T(8,128)} %get-tuple-element.11.gate, s32[784,1]{1,0:T(8,128)} %get-tuple-element.12.key), custom_call_target="tpu_custom_call" | custom-call | tf_op jit(solution)/shard_map/combine/pallas_call | solution.py:322

commit v2 on v0

v2 whole, which is shorter than its diff:
```python
import itertools

import jax
import jax.numpy as jnp
from jax import lax
from jax.experimental import pallas as pl
from jax.experimental.pallas import tpu as pltpu
from jax.sharding import PartitionSpec as P

MESH = pl.DeviceIdType.MESH
SIDE = 4
LANES = 128
PLACES = sorted(
    itertools.product(range(SIDE), repeat=3),
    key=lambda o: (o != (0, 0, 0), (o[0] * 7 + o[1] * 11 + o[2] * 13) % 16),
)
CHUNK = 16
HIGH = 16 * CHUNK
SLOTS = 19 * CHUNK
CHUNKS = len(PLACES) // CHUNK
F32 = jnp.float32
BF16 = jnp.bfloat16


def iota(shape, dim):
    return lax.broadcasted_iota(jnp.int32, shape, dim)


def layer_kernel(
    patches, visible, route, cap, gain, bias, router, w_in, b_in, w_out, b_out, out,
    store, sent, got, made, back, w1, w2, rows, act, tail, rest, picked, hb, ordered, gate, sel, total,
    load_sem, s_sem, r_sem, ys_sem, yr_sem,
):
    images, width = store.shape[1], store.shape[2]
    keep = visible.shape[1]
    toks = images * keep
    experts = cap.shape[1]
    hidden = w1.shape[1]
    me = lax.axis_index("expert")
    mx, my, mz = me // (SIDE * SIDE), (me // SIDE) % SIDE, me % SIDE

    def at(o, sign):
        x = (mx + sign * o[0] + SIDE) % SIDE
        y = (my + sign * o[1] + SIDE) % SIDE
        z = (mz + sign * o[2] + SIDE) % SIDE
        return (x * SIDE + y) * SIDE + z

    load = pltpu.make_async_copy(patches, store, load_sem.at[0])
    load.start()
    barrier = pltpu.get_barrier_semaphore()
    for o in PLACES[1:]:
        pl.semaphore_signal(barrier, inc=1, device_id={"expert": at(o, 1)}, device_id_type=MESH)

    def place(shape, dim):
        t = iota(shape, dim)
        return (t % images) * keep + t // images

    def slot_of(block, rank):
        j = block % CHUNK
        inside = jnp.where(
            rank < 8,
            j * 8 + rank,
            jnp.where(rank < 16, 8 * CHUNK + j * 8 + rank - 8, rank * CHUNK + j),
        )
        return (block // CHUNK) * SLOTS + inside

    block_col = jnp.zeros((experts, 1), jnp.int32)
    block_row = jnp.zeros((1, experts), jnp.int32)
    for i, o in enumerate(PLACES):
        where = at(o, 1)
        block_col = jnp.where(iota((experts, 1), 0) == where, i, block_col)
        block_row = jnp.where(iota((1, experts), 1) == where, i, block_row)

    diag = iota((experts, experts), 0) == iota((experts, experts), 1)
    cap_col = jnp.sum(jnp.where(diag, cap[...], 0), axis=1, keepdims=True)
    route_b = jnp.broadcast_to(route[...], (8, toks)).astype(F32).astype(BF16)
    to_picked = (iota((toks, 1), 0) == place((1, toks), 1)).astype(BF16)
    route_p = jnp.dot(route_b, to_picked, preferred_element_type=F32)[:1].astype(jnp.int32)
    one_row = iota((experts, toks), 0) == route_p
    ones = one_row.astype(F32)
    earlier = (place((toks, 1), 0) < place((1, toks), 1)).astype(BF16)
    before = jnp.dot(ones.astype(BF16), earlier, preferred_element_type=F32)
    rank = jnp.sum(before * ones, axis=0, keepdims=True).astype(jnp.int32)
    limit = jnp.sum(jnp.where(one_row, cap_col, 0), axis=0, keepdims=True)
    block = jnp.sum(jnp.where(one_row, block_col, 0), axis=0, keepdims=True)
    key = jnp.where(rank < limit, slot_of(block, rank), -1)

    load.wait()
    load1 = pltpu.make_async_copy(w_in.at[0], w1, load_sem.at[1])
    load1.start()
    load2 = pltpu.make_async_copy(w_out.at[0], w2, load_sem.at[2])
    load2.start()

    row = iota((images, width), 0)

    def pick(k, carry):
        val = store[visible[0, k]]
        for i in range(1, images):
            val = jnp.where(row == i, store[visible[i, k]], val)
        picked[pl.ds(pl.multiple_of(k * images, images), images), :] = val
        return carry

    lax.fori_loop(0, keep, pick, 0, unroll=7)

    def normed(xf):
        mean = jnp.sum(xf, axis=1, keepdims=True) * (1.0 / width)
        diff = xf - mean
        var = jnp.sum(diff * diff, axis=1, keepdims=True) * (1.0 / width)
        return diff * (1.0 / jnp.sqrt(var + 1e-06)) * gain[...] + bias[...]

    def norm(k, carry):
        span = pl.ds(pl.multiple_of(k * images, images), images)
        hb[span, :] = normed(picked[span, :].astype(F32)).astype(BF16)
        return carry

    lax.fori_loop(0, keep, norm, 0, unroll=7)

    def out_copy(i):
        return pltpu.make_async_remote_copy(
            src_ref=sent.at[i], dst_ref=got.at[i], send_sem=s_sem.at[i], recv_sem=r_sem.at[i],
            device_id={"expert": at(PLACES[i], 1)}, device_id_type=MESH,
        )

    def back_copy(i):
        return pltpu.make_async_remote_copy(
            src_ref=made.at[i], dst_ref=back.at[i], send_sem=ys_sem.at[i], recv_sem=yr_sem.at[i],
            device_id={"expert": at(PLACES[i], -1)}, device_id_type=MESH,
        )

    half = 8 * CHUNK

    def put(ref, lo, y, cols, start):
        wide = y.shape[1]
        for part in range(2):
            lanes = pl.ds(pl.multiple_of(part * width + start, wide), wide)
            ref[lo : lo + CHUNK, :, lanes] = (
                y[part * half : (part + 1) * half].reshape(CHUNK, 8, wide).astype(BF16)
            )
        rest[:, cols] = y[HIGH:]

    def put_rest(ref, lo):
        for r in range(3):
            for j in range(8):
                tail[r, pl.ds(j, CHUNK, stride=8), :] = rest[
                    r * CHUNK : (r + 1) * CHUNK, j * LANES : (j + 1) * LANES
                ]
            lanes = slice(2 * width + r * LANES, 2 * width + (r + 1) * LANES)
            ref[lo : lo + CHUNK, :, lanes] = tail[r].reshape(CHUNK, 8, LANES).astype(BF16)

    def take(ref, lo):
        for part in range(2):
            piece = ref[lo : lo + CHUNK, :, part * width : (part + 1) * width]
            rows[part * half : (part + 1) * half, :] = (
                piece.astype(F32).reshape(half, width).astype(BF16)
            )
        for r in range(3):
            lanes = slice(2 * width + r * LANES, 2 * width + (r + 1) * LANES)
            tail[r] = ref[lo : lo + CHUNK, :, lanes].astype(F32).reshape(half, LANES)
            for j in range(8):
                first = HIGH + r * CHUNK
                rows[first : first + CHUNK, j * LANES : (j + 1) * LANES] = tail[
                    r, pl.ds(j, CHUNK, stride=8), :
                ].astype(BF16)

    wide = 256
    for c in range(CHUNKS):
        lo = c * CHUNK
        chosen = (iota((SLOTS, toks), 0) + c * SLOTS == key).astype(BF16)
        for n in range(width // wide):
            cols = slice(n * wide, (n + 1) * wide)
            y = jnp.dot(chosen, hb[:, cols], preferred_element_type=F32)
            put(sent, lo, y, cols, n * wide)
        put_rest(sent, lo)
        if c == 0:
            pl.semaphore_wait(barrier, len(PLACES) - 1)
        for i in range(max(lo, 1), lo + CHUNK):
            out_copy(i).start()
        if c == 0:
            got[0] = sent[0]

    to_own = (place((1, toks), 1) == iota((toks, 1), 0)).astype(BF16)
    for n in range(width // wide):
        cols = slice(n * wide, (n + 1) * wide)
        ordered[:, cols] = jnp.dot(to_own, picked[:, cols], preferred_element_type=F32).astype(BF16)
    eye = (iota((toks, 1), 0) == iota((1, toks), 1)).astype(BF16)
    route_c = lax.dot_general(
        eye, route_b, (((1,), (1,)), ((), ())), preferred_element_type=F32
    )[:, :1].astype(jnp.int32)
    one_col = iota((toks, experts), 1) == route_c
    ones_c = one_col.astype(F32)
    lower = (iota((toks, 1), 0) > iota((1, toks), 1)).astype(BF16)
    before_c = jnp.dot(lower, ones_c.astype(BF16), preferred_element_type=F32)
    rank_c = jnp.sum(before_c * ones_c, axis=1, keepdims=True).astype(jnp.int32)
    limit_c = jnp.sum(jnp.where(one_col, cap[...], 0), axis=1, keepdims=True)
    block_c = jnp.sum(jnp.where(one_col, block_row, 0), axis=1, keepdims=True)
    key_c = jnp.where(rank_c < limit_c, slot_of(block_c, rank_c), -1)
    for c in range(CHUNKS):
        sel[c] = (iota((toks, SLOTS), 1) + c * SLOTS == key_c).astype(BF16)

    r_full = router[...]
    r_hi = r_full.astype(BF16)
    r_lo = (r_full - r_hi.astype(F32)).astype(BF16)

    def product(a, b):
        return lax.dot_general(a, b, (((1,), (1,)), ((), ())), preferred_element_type=F32)

    group = 7 * images
    for g in range(toks // group):
        span = slice(g * group, (g + 1) * group)
        h = normed(ordered[span, :].astype(F32))
        h_hi = h.astype(BF16)
        h_lo = (h - h_hi.astype(F32)).astype(BF16)
        logits = product(h_hi, r_lo) + product(h_lo, r_hi) + product(h_hi, r_hi)
        score = jnp.sum(logits * ones_c[span], axis=1, keepdims=True)
        gate[span, :] = jnp.broadcast_to(1.0 / (1.0 + jnp.exp(-score)), (group, LANES))

    step = 512

    def gather_back(c):
        lo = c * CHUNK
        for i in range(max(lo, 1), lo + CHUNK):
            back_copy(i).wait_recv()
        take(back, lo)
        for n in range(width // wide):
            cols = slice(n * wide, (n + 1) * wide)
            part = jnp.dot(sel[c], rows[:, cols], preferred_element_type=F32)
            if c > 0:
                part = part + total[:, cols]
            if c < CHUNKS - 1:
                total[:, cols] = part
            else:
                out[:, cols] = (ordered[:, cols].astype(F32) + gate[:, :1] * part).astype(BF16)

    for c in range(CHUNKS):
        lo = c * CHUNK
        for i in range(max(lo, 1), lo + CHUNK):
            out_copy(i).wait_recv()
        take(got, lo)
        if c == 0:
            load1.wait()
            load2.wait()

        @pl.loop(0, hidden // step)
        def _(f):
            cols = pl.ds(pl.multiple_of(f * step, step), step)
            v = jnp.dot(rows[...], w1[:, cols], preferred_element_type=F32) + b_in[:, cols]
            inner = v * (0.7978845608028654 + 0.035677408136300125 * (v * v))
            half_v = 0.5 * v
            act[:, cols] = (half_v + half_v * jnp.tanh(inner)).astype(BF16)

        @pl.loop(0, width // wide)
        def _(n):
            start = n * wide
            cols = pl.ds(pl.multiple_of(start, wide), wide)
            y = jnp.dot(act[...], w2[:, cols], preferred_element_type=F32) + b_out[:, cols]
            put(made, lo, y, cols, start)

        put_rest(made, lo)
        for i in range(max(lo, 1), lo + CHUNK):
            back_copy(i).start()
        if c == 0:
            back[0] = made[0]
        if c >= 2:
            gather_back(c - 2)
    for i in range(1, len(PLACES)):
        out_copy(i).wait_send()
    gather_back(CHUNKS - 2)
    gather_back(CHUNKS - 1)
    for i in range(1, len(PLACES)):
        back_copy(i).wait_send()


def per_device(
    patches, visible, routes, expert_cap, norm_gain, norm_bias, router, w_in, b_in, w_out, b_out
):
    images, _, width = patches.shape
    toks = images * visible.shape[1]
    experts = expert_cap.shape[0]
    hidden = w_in.shape[2]
    by_patch = jnp.transpose(patches, (1, 0, 2))
    vmem = pl.BlockSpec(memory_space=pltpu.VMEM)
    smem = pl.BlockSpec(memory_space=pltpu.SMEM)
    any_ = pl.BlockSpec(memory_space=pl.ANY)
    blk = (experts, 8, 2 * width + 3 * LANES)
    dma = pltpu.SemaphoreType.DMA
    return pl.pallas_call(
        layer_kernel,
        out_shape=jax.ShapeDtypeStruct((toks, width), BF16),
        in_specs=[any_, smem] + [vmem] * 5 + [any_, vmem, any_, vmem],
        out_specs=vmem,
        scratch_shapes=[
            pltpu.VMEM(by_patch.shape, BF16),
            pltpu.VMEM(blk, BF16),
            pltpu.VMEM(blk, BF16),
            pltpu.VMEM(blk, BF16),
            pltpu.VMEM(blk, BF16),
            pltpu.VMEM((width, hidden), BF16),
            pltpu.VMEM((hidden, width), BF16),
            pltpu.VMEM((SLOTS, width), BF16),
            pltpu.VMEM((SLOTS, hidden), BF16),
            pltpu.VMEM((3, 8 * CHUNK, LANES), F32),
            pltpu.VMEM((3 * CHUNK, width), F32),
            pltpu.VMEM((toks, width), BF16),
            pltpu.VMEM((toks, width), BF16),
            pltpu.VMEM((toks, width), BF16),
            pltpu.VMEM((toks, LANES), F32),
            pltpu.VMEM((CHUNKS, toks, SLOTS), BF16),
            pltpu.VMEM((toks, width), F32),
            dma((3,)),
            dma((experts,)),
            dma((experts,)),
            dma((experts,)),
            dma((experts,)),
        ],
        compiler_params=pltpu.CompilerParams(
            collective_id=0, has_side_effects=True, vmem_limit_bytes=63 * 2**20
        ),
        name="layer",
    )(
        by_patch, visible, routes.reshape(1, toks), expert_cap.reshape(1, experts),
        norm_gain.reshape(1, width), norm_bias.reshape(1, width), router.T, w_in, b_in, w_out, b_out,
    )


def solution(mesh):
    return jax.shard_map(
        per_device,
        mesh=mesh,
        in_specs=(
            P(("dp", "expert"), None, None),
            P(("dp", "expert"), None),
            P(("dp", "expert"), None),
            P("dp"),
            P(),
            P(),
            P(),
            P("expert", None, None),
            P("expert", None),
            P("expert", None, None),
            P("expert", None),
        ),
        out_specs=P(("dp", "expert"), None),
        check_vma=False,
    )
```

time: 191 us -> 88.6 us (0.46)
  the two profiles are of different devices: /device:TPU:0 before, /device:TPU:4 now
where the time goes in v2:
time: 88.6 us; the launch traced here: 88.5 us
  Pallas kernels  85.7 us (97%)
  local copies, waits for them, and re-layouts  2.69 us (3%)
    pallas_call x1, Pallas kernels, per_device(): pl.pallas_call(layer_kernel, out_shape=jax.ShapeDtypeStruct((toks, width)...  85.7 us
    unnamed x1, local copies, waits for them, and re-layouts  2.69 us

profile of v2, /device:TPU:4, one launch (start us, length us, event | category | flops | bytes accessed | tf_op | source)
XLA Modules:
  0.0 88.5 jit_solution(11867756517771589779)
XLA Ops:
  0.0 85.7 %layer.1 = bf16[784,1024]{1,0:T(8,128)(2,1)} custom-call(bf16[196,16,1024]{2,1,0:T(8,128)(2,1)} %bitcast.6, s32[16,49]{1,0:T(8,128)} %visible.1, s32[1,784]{1,0:T(1,128)} %bitcast.10, s32[1,64]{1,0:T(1,128)} %bitcast.11, f32[1,1024]{1,0:T(1,128)} %bitcast.8, f32[1,1024]{1,0:T(1,128)} %bitcast.9, f32[64,1024]{1,0:T(8,128)} %bitcast.7, ...), custom_call_target="tpu_custom_call" | custom-call | tf_op jit(solution)/shard_map/layer/pallas_call | solution.py:286
  85.8 2.7 %copy.13 = bf16[784,1024]{1,0:T(8,128)(2,1)} copy(bf16[784,1024]{1,0:T(8,128)(2,1)} %layer.1) | data formatting | bytes 3211264

commit v3 on v2

v3 whole, which is shorter than its diff:
```python
import jax
import jax.numpy as jnp
from jax import lax
from jax.experimental import pallas as pl
from jax.experimental.pallas import tpu as pltpu
from jax.sharding import PartitionSpec as P

MESH = pl.DeviceIdType.MESH
SIDE = 4
LANES = 128
PARTNERS = SIDE**3
TURN = 37
BACKTURN = 45
CHUNK = 16
HIGH = 16 * CHUNK
SLOTS = 19 * CHUNK
CHUNKS = PARTNERS // CHUNK
F32 = jnp.float32
BF16 = jnp.bfloat16


def iota(shape, dim):
    return lax.broadcasted_iota(jnp.int32, shape, dim)


def layer_kernel(
    patches, visible, route, cap, gain, bias, router, w_in, b_in, w_out, b_out, out,
    store, sent, got, made, back, w1, w2, rows, act, even, odd, tail, picked, hb, ordered, gate, sel,
    total, load_sem, s_sem, r_sem, ys_sem, yr_sem,
):
    images, width = store.shape[1], store.shape[2]
    keep = visible.shape[1]
    toks = images * keep
    experts = cap.shape[1]
    hidden = w1.shape[1]
    me = lax.axis_index("expert")
    mx, my, mz = me // (SIDE * SIDE), (me // SIDE) % SIDE, me % SIDE

    def partner(i, sign):
        code = (i * TURN) % PARTNERS
        x = (mx + sign * (code // (SIDE * SIDE)) + SIDE) % SIDE
        y = (my + sign * ((code // SIDE) % SIDE) + SIDE) % SIDE
        z = (mz + sign * (code % SIDE) + SIDE) % SIDE
        return (x * SIDE + y) * SIDE + z

    load = pltpu.make_async_copy(patches, store, load_sem.at[0])
    load.start()
    barrier = pltpu.get_barrier_semaphore()
    for i in range(1, PARTNERS):
        pl.semaphore_signal(barrier, inc=1, device_id={"expert": partner(i, 1)}, device_id_type=MESH)

    def place(shape, dim):
        t = iota(shape, dim)
        return (t % images) * keep + t // images

    def slot_of(block, rank):
        j = block % CHUNK
        inside = jnp.where(
            rank < 8,
            j * 8 + rank,
            jnp.where(rank < 16, 8 * CHUNK + j * 8 + rank - 8, rank * CHUNK + j),
        )
        return (block // CHUNK) * SLOTS + inside

    def block_of(expert):
        x = (expert // (SIDE * SIDE) - mx + SIDE) % SIDE
        y = ((expert // SIDE) % SIDE - my + SIDE) % SIDE
        z = (expert % SIDE - mz + SIDE) % SIDE
        return (((x * SIDE + y) * SIDE + z) * BACKTURN) % PARTNERS

    diag = iota((experts, experts), 0) == iota((experts, experts), 1)
    cap_col = jnp.sum(jnp.where(diag, cap[...], 0), axis=1, keepdims=True)
    route_b = jnp.broadcast_to(route[...], (8, toks)).astype(F32).astype(BF16)
    to_picked = (iota((toks, 1), 0) == place((1, toks), 1)).astype(BF16)
    route_p = jnp.dot(route_b, to_picked, preferred_element_type=F32)[:1].astype(jnp.int32)
    one_row = iota((experts, toks), 0) == route_p
    ones = one_row.astype(F32)
    earlier = (place((toks, 1), 0) < place((1, toks), 1)).astype(BF16)
    before = jnp.dot(ones.astype(BF16), earlier, preferred_element_type=F32)
    rank = jnp.sum(before * ones, axis=0, keepdims=True).astype(jnp.int32)
    limit = jnp.sum(jnp.where(one_row, cap_col, 0), axis=0, keepdims=True)
    key = jnp.where(rank < limit, slot_of(block_of(route_p), rank), -1)

    load.wait()
    load1 = pltpu.make_async_copy(w_in.at[0], w1, load_sem.at[1])
    load1.start()
    load2 = pltpu.make_async_copy(w_out.at[0], w2, load_sem.at[2])
    load2.start()

    row = iota((images, width), 0)

    def pick(k, carry):
        val = store[visible[0, k]]
        for i in range(1, images):
            val = jnp.where(row == i, store[visible[i, k]], val)
        picked[pl.ds(pl.multiple_of(k * images, images), images), :] = val
        return carry

    lax.fori_loop(0, keep, pick, 0, unroll=7)

    def normed(xf):
        mean = jnp.sum(xf, axis=1, keepdims=True) * (1.0 / width)
        diff = xf - mean
        var = jnp.sum(diff * diff, axis=1, keepdims=True) * (1.0 / width)
        return diff * (1.0 / jnp.sqrt(var + 1e-06)) * gain[...] + bias[...]

    def norm(k, carry):
        span = pl.ds(pl.multiple_of(k * images, images), images)
        hb[span, :] = normed(picked[span, :].astype(F32)).astype(BF16)
        return carry

    lax.fori_loop(0, keep, norm, 0, unroll=7)

    def out_copy(i):
        return pltpu.make_async_remote_copy(
            src_ref=sent.at[i], dst_ref=got.at[i], send_sem=s_sem.at[i], recv_sem=r_sem.at[i],
            device_id={"expert": partner(i, 1)}, device_id_type=MESH,
        )

    def back_copy(i):
        return pltpu.make_async_remote_copy(
            src_ref=made.at[i], dst_ref=back.at[i], send_sem=ys_sem.at[i], recv_sem=yr_sem.at[i],
            device_id={"expert": partner(i, -1)}, device_id_type=MESH,
        )

    half = 8 * CHUNK

    def each(c, act_on):
        @pl.when(c > 0)
        def _():
            act_on(c * CHUNK)

        for i in range(1, CHUNK):
            act_on(c * CHUNK + i)

    def put(ref, lo, y):
        span = pl.ds(lo, CHUNK)
        for part in range(2):
            ref[span, :, part * width : (part + 1) * width] = (
                y[part * half : (part + 1) * half].reshape(CHUNK, 8, width).astype(BF16)
            )
        for r in range(3):
            first = HIGH + r * CHUNK
            for j in range(8):
                tail[r, pl.ds(j, CHUNK, stride=8), :] = y[
                    first : first + CHUNK, j * LANES : (j + 1) * LANES
                ]
            lanes = slice(2 * width + r * LANES, 2 * width + (r + 1) * LANES)
            ref[span, :, lanes] = tail[r].reshape(CHUNK, 8, LANES).astype(BF16)

    def take(ref, lo):
        span = pl.ds(lo, CHUNK)
        for part in range(2):
            piece = ref[span, :, part * width : (part + 1) * width]
            rows[part * half : (part + 1) * half, :] = (
                piece.astype(F32).reshape(half, width).astype(BF16)
            )
        for r in range(3):
            lanes = slice(2 * width + r * LANES, 2 * width + (r + 1) * LANES)
            tail[r] = ref[span, :, lanes].astype(F32).reshape(half, LANES)
            for j in range(8):
                first = HIGH + r * CHUNK
                rows[first : first + CHUNK, j * LANES : (j + 1) * LANES] = tail[
                    r, pl.ds(j, CHUNK, stride=8), :
                ].astype(BF16)

    @pl.loop(0, CHUNKS)
    def _(c):
        chosen = (iota((SLOTS, toks), 0) + c * SLOTS == key).astype(BF16)
        put(sent, c * CHUNK, jnp.dot(chosen, hb[...], preferred_element_type=F32))

        @pl.when(c == 0)
        def _():
            pl.semaphore_wait(barrier, PARTNERS - 1)
            got[0] = sent[0]

        each(c, lambda i: out_copy(i).start())

    total[...] = jnp.zeros_like(total)
    to_own = (place((1, toks), 1) == iota((toks, 1), 0)).astype(BF16)
    ordered[...] = jnp.dot(to_own, picked[...], preferred_element_type=F32).astype(BF16)
    eye = (iota((toks, 1), 0) == iota((1, toks), 1)).astype(BF16)

    def product(a, b):
        return lax.dot_general(a, b, (((1,), (1,)), ((), ())), preferred_element_type=F32)

    route_c = product(eye, route_b)[:, :1].astype(jnp.int32)
    one_col = iota((toks, experts), 1) == route_c
    ones_c = one_col.astype(F32)
    lower = (iota((toks, 1), 0) > iota((1, toks), 1)).astype(BF16)
    before_c = jnp.dot(lower, ones_c.astype(BF16), preferred_element_type=F32)
    rank_c = jnp.sum(before_c * ones_c, axis=1, keepdims=True).astype(jnp.int32)
    limit_c = jnp.sum(jnp.where(one_col, cap[...], 0), axis=1, keepdims=True)
    block_c = jnp.sum(
        jnp.where(one_col, block_of(iota((1, experts), 1)), 0), axis=1, keepdims=True
    )
    key_c = jnp.where(rank_c < limit_c, slot_of(block_c, rank_c), -1)
    for c in range(CHUNKS):
        sel[c] = (iota((toks, SLOTS), 1) + c * SLOTS == key_c).astype(BF16)

    r_full = router[...]
    r_hi = r_full.astype(BF16)
    r_lo = (r_full - r_hi.astype(F32)).astype(BF16)
    group = 7 * images
    for g in range(toks // group):
        span = slice(g * group, (g + 1) * group)
        h = normed(ordered[span, :].astype(F32))
        h_hi = h.astype(BF16)
        h_lo = (h - h_hi.astype(F32)).astype(BF16)
        logits = product(h_hi, r_lo) + product(h_lo, r_hi) + product(h_hi, r_hi)
        score = jnp.sum(logits * ones_c[span], axis=1, keepdims=True)
        gate[span, :] = jnp.broadcast_to(1.0 / (1.0 + jnp.exp(-score)), (group, LANES))

    step = 1024
    last = hidden - step

    def enter(f, ref):
        ref[...] = jnp.dot(rows[...], w1[:, f : f + step], preferred_element_type=F32)

    def bend(f, ref):
        v = ref[...] + b_in[:, f : f + step]
        inner = v * (0.7978845608028654 + 0.035677408136300125 * (v * v))
        half_v = 0.5 * v
        act[:, f : f + step] = (half_v + half_v * jnp.tanh(inner)).astype(BF16)

    load1.wait()
    load2.wait()

    @pl.loop(0, CHUNKS)
    def _(c):
        each(c, lambda i: out_copy(i).wait_recv())
        take(got, c * CHUNK)
        spare = (even, odd)
        enter(0, even)
        for n in range(1, hidden // step):
            enter(n * step, spare[n % 2])
            bend((n - 1) * step, spare[(n - 1) % 2])
        y = jnp.dot(act[:, :last], w2[:last, :], preferred_element_type=F32)
        bend(last, spare[(hidden // step - 1) % 2])
        y = y + jnp.dot(act[:, last:], w2[last:, :], preferred_element_type=F32)
        put(made, c * CHUNK, y + b_out[...])
        each(c, lambda i: back_copy(i).start())

        @pl.when(c == 0)
        def _():
            back[0] = made[0]

        @pl.when(c >= 2)
        def _():
            each(c - 2, lambda i: back_copy(i).wait_recv())
            take(back, (c - 2) * CHUNK)
            total[...] += jnp.dot(sel[c - 2], rows[...], preferred_element_type=F32)

    @pl.loop(1, PARTNERS)
    def _(i):
        out_copy(i).wait_send()

    c = CHUNKS - 2
    each(c, lambda i: back_copy(i).wait_recv())
    take(back, c * CHUNK)
    total[...] += jnp.dot(sel[c], rows[...], preferred_element_type=F32)
    c = CHUNKS - 1
    each(c, lambda i: back_copy(i).wait_recv())
    take(back, c * CHUNK)
    wide = width // 2
    writes = []
    for n in range(2):
        cols = slice(n * wide, (n + 1) * wide)
        part = total[:, cols] + jnp.dot(sel[c], rows[:, cols], preferred_element_type=F32)
        hb[:, cols] = (ordered[:, cols].astype(F32) + gate[:, :1] * part).astype(BF16)
        writes.append(pltpu.make_async_copy(hb.at[:, cols], out.at[:, cols], load_sem.at[n]))
        writes[-1].start()

    @pl.loop(1, PARTNERS)
    def _(i):
        back_copy(i).wait_send()

    for write in writes:
        write.wait()


def finish_kernel(src, out, buf, in_sem, out_sem):
    rows = src.shape[0]
    size = rows // in_sem.shape[0]
    pieces = [pl.ds(n * size, size) for n in range(in_sem.shape[0])]
    loads = [pltpu.make_async_copy(src.at[p], buf.at[p], in_sem.at[n]) for n, p in enumerate(pieces)]
    stores = [pltpu.make_async_copy(buf.at[p], out.at[p], out_sem.at[n]) for n, p in enumerate(pieces)]
    for copy in loads:
        copy.start()
    for n, copy in enumerate(stores):
        loads[n].wait()
        copy.start()
    for copy in stores:
        copy.wait()


def per_device(
    patches, visible, routes, expert_cap, norm_gain, norm_bias, router, w_in, b_in, w_out, b_out
):
    images, _, width = patches.shape
    toks = images * visible.shape[1]
    experts = expert_cap.shape[0]
    hidden = w_in.shape[2]
    by_patch = jnp.transpose(patches, (1, 0, 2))
    vmem = pl.BlockSpec(memory_space=pltpu.VMEM)
    smem = pl.BlockSpec(memory_space=pltpu.SMEM)
    any_ = pl.BlockSpec(memory_space=pl.ANY)
    blk = (experts, 8, 2 * width + 3 * LANES)
    dma = pltpu.SemaphoreType.DMA
    done = jax.ShapeDtypeStruct((toks, width), BF16)
    result = pl.pallas_call(
        layer_kernel,
        out_shape=done,
        in_specs=[any_, smem] + [vmem] * 5 + [any_, vmem, any_, vmem],
        out_specs=any_,
        scratch_shapes=[
            pltpu.VMEM(by_patch.shape, BF16),
            pltpu.VMEM(blk, BF16),
            pltpu.VMEM(blk, BF16),
            pltpu.VMEM(blk, BF16),
            pltpu.VMEM(blk, BF16),
            pltpu.VMEM((width, hidden), BF16),
            pltpu.VMEM((hidden, width), BF16),
            pltpu.VMEM((SLOTS, width), BF16),
            pltpu.VMEM((SLOTS, hidden), BF16),
            pltpu.VMEM((SLOTS, 1024), F32),
            pltpu.VMEM((SLOTS, 1024), F32),
            pltpu.VMEM((3, 8 * CHUNK, LANES), F32),
            pltpu.VMEM((toks, width), BF16),
            pltpu.VMEM((toks, width), BF16),
            pltpu.VMEM((toks, width), BF16),
            pltpu.VMEM((toks, LANES), F32),
            pltpu.VMEM((CHUNKS, toks, SLOTS), BF16),
            pltpu.VMEM((toks, width), F32),
            dma((3,)),
            dma((experts,)),
            dma((experts,)),
            dma((experts,)),
            dma((experts,)),
        ],
        compiler_params=pltpu.CompilerParams(
            collective_id=0, has_side_effects=True, vmem_limit_bytes=63 * 2**20
        ),
        name="layer",
    )(
        by_patch, visible, routes.reshape(1, toks), expert_cap.reshape(1, experts),
        norm_gain.reshape(1, width), norm_bias.reshape(1, width), router.T, w_in, b_in, w_out, b_out,
    )
    pieces = 7
    return pl.pallas_call(
        finish_kernel,
        out_shape=done,
        in_specs=[any_],
        out_specs=any_,
        scratch_shapes=[pltpu.VMEM((toks, width), BF16), dma((pieces,)), dma((pieces,))],
        name="finish",
    )(result)


def solution(mesh):
    return jax.shard_map(
        per_device,
        mesh=mesh,
        in_specs=(
            P(("dp", "expert"), None, None),
            P(("dp", "expert"), None),
            P(("dp", "expert"), None),
            P("dp"),
            P(),
            P(),
            P(),
            P("expert", None, None),
            P("expert", None),
            P("expert", None, None),
            P("expert", None),
        ),
        out_specs=P(("dp", "expert"), None),
        check_vma=False,
    )
```

time: 88.6 us -> 78.9 us (0.89)
  the two profiles are of different devices: /device:TPU:4 before, /device:TPU:0 now
where the time goes in v3:
time: 78.9 us; the launch traced here: 77.9 us
  Pallas kernels  77.7 us (98%)
    pallas_call x1, Pallas kernels, per_device(): pl.pallas_call(layer_kernel, out_shape=done, in_specs=[any_, smem] + [vme...  75.4 us
    pallas_call x1, Pallas kernels, per_device(): pl.pallas_call(finish_kernel, out_shape=done, in_specs=[any_], out_specs=...  2.32 us

profile of v3, /device:TPU:0, one launch (start us, length us, event | category | flops | bytes accessed | tf_op | source)
XLA Modules:
  0.0 77.9 jit_solution(9148724461279163027)
XLA Ops:
  0.0 75.4 %layer.1.src = bf16[784,1024]{1,0:T(8,128)(2,1)} custom-call(bf16[196,16,1024]{2,1,0:T(8,128)(2,1)} %bitcast.6, s32[16,49]{1,0:T(8,128)} %visible.1, s32[1,784]{1,0:T(1,128)} %bitcast.10, s32[1,64]{1,0:T(1,128)} %bitcast.11, f32[1,1024]{1,0:T(1,128)} %bitcast.8, f32[1,1024]{1,0:T(1,128)} %bitcast.9, f32[64,1024]{1,0:T(8,128)} %bitcast.7, ...), custom_call_target="tpu_custom_call" | custom-call | tf_op jit(solution)/shard_map/layer/pallas_call | solution.py:311
  75.4 2.3 %finish.1 = bf16[784,1024]{1,0:T(8,128)(2,1)} custom-call(bf16[784,1024]{1,0:T(8,128)(2,1)} %layer.1.src), custom_call_target="tpu_custom_call" | custom-call | tf_op jit(solution)/shard_map/finish/pallas_call | solution.py:350

commit v4 on v3

--- a/solution.py
+++ b/solution.py
@@ -24,11 +24,12 @@
 
 
 def layer_kernel(
-    patches, visible, route, cap, gain, bias, router, w_in, b_in, w_out, b_out, out,
-    store, sent, got, made, back, w1, w2, rows, act, even, odd, tail, picked, hb, ordered, gate, sel,
-    total, load_sem, s_sem, r_sem, ys_sem, yr_sem,
+    patches, visible_in, route_in, cap_in, gain_in, bias_in, router_in, w_in, b_in_in, w_out, b_out_in,
+    out, store_a, store_b, visible, route, cap, gain, bias, router, b_in, b_out, sent, got, made, back, w1, w2,
+    rows, act, even, odd, tail, picked, ordered, gate, sel, total,
+    load_sem, s_sem, r_sem, ys_sem, yr_sem,
 ):
-    images, width = store.shape[1], store.shape[2]
+    images, width = patches.shape[1], patches.shape[2]
     keep = visible.shape[1]
     toks = images * keep
     experts = cap.shape[1]
@@ -43,8 +44,26 @@
         z = (mz + sign * (code % SIDE) + SIDE) % SIDE
         return (x * SIDE + y) * SIDE + z
 
-    load = pltpu.make_async_copy(patches, store, load_sem.at[0])
-    load.start()
+    small = [
+        pltpu.make_async_copy(src, dst, load_sem.at[n])
+        for n, (src, dst) in enumerate(
+            (
+                (route_in, route), (cap_in, cap), (visible_in, visible), (gain_in, gain),
+                (bias_in, bias), (router_in, router), (b_in_in, b_in), (b_out_in, b_out),
+            )
+        )
+    ]
+    split = width // 2
+    load = [
+        pltpu.make_async_copy(
+            patches.at[:, :, n * split : (n + 1) * split],
+            store,
+            load_sem.at[len(small) + n],
+        )
+        for n, store in enumerate((store_a, store_b))
+    ]
+    for copy in small[:3] + load + small[3:]:
+        copy.start()
     barrier = pltpu.get_barrier_semaphore()
     for i in range(1, PARTNERS):
         pl.semaphore_signal(barrier, inc=1, device_id={"expert": partner(i, 1)}, device_id_type=MESH)
@@ -68,6 +87,8 @@
         z = (expert % SIDE - mz + SIDE) % SIDE
         return (((x * SIDE + y) * SIDE + z) * BACKTURN) % PARTNERS
 
+    small[0].wait()
+    small[1].wait()
     diag = iota((experts, experts), 0) == iota((experts, experts), 1)
     cap_col = jnp.sum(jnp.where(diag, cap[...], 0), axis=1, keepdims=True)
     route_b = jnp.broadcast_to(route[...], (8, toks)).astype(F32).astype(BF16)
@@ -81,35 +102,30 @@
     limit = jnp.sum(jnp.where(one_row, cap_col, 0), axis=0, keepdims=True)
     key = jnp.where(rank < limit, slot_of(block_of(route_p), rank), -1)
 
-    load.wait()
-    load1 = pltpu.make_async_copy(w_in.at[0], w1, load_sem.at[1])
+    small[2].wait()
+    row = iota((images, split), 0)
+    for n, store in enumerate((store_a, store_b)):
+        load[n].wait()
+
+        def pick(k, carry, store=store, lanes=slice(n * split, (n + 1) * split)):
+            val = store[visible[0, k]]
+            for i in range(1, images):
+                val = jnp.where(row == i, store[visible[i, k]], val)
+            picked[pl.ds(pl.multiple_of(k * images, images), images), lanes] = val
+            return carry
+
+        lax.fori_loop(0, keep, pick, 0, unroll=7)
+
+    load1 = pltpu.make_async_copy(w_in.at[0], w1, load_sem.at[10])
     load1.start()
-    load2 = pltpu.make_async_copy(w_out.at[0], w2, load_sem.at[2])
+    load2 = pltpu.make_async_copy(w_out.at[0], w2, load_sem.at[11])
     load2.start()
-
-    row = iota((images, width), 0)
-
-    def pick(k, carry):
-        val = store[visible[0, k]]
-        for i in range(1, images):
-            val = jnp.where(row == i, store[visible[i, k]], val)
-        picked[pl.ds(pl.multiple_of(k * images, images), images), :] = val
-        return carry
-
-    lax.fori_loop(0, keep, pick, 0, unroll=7)
 
     def normed(xf):
         mean = jnp.sum(xf, axis=1, keepdims=True) * (1.0 / width)
         diff = xf - mean
         var = jnp.sum(diff * diff, axis=1, keepdims=True) * (1.0 / width)
         return diff * (1.0 / jnp.sqrt(var + 1e-06)) * gain[...] + bias[...]
-
-    def norm(k, carry):
-        span = pl.ds(pl.multiple_of(k * images, images), images)
-        hb[span, :] = normed(picked[span, :].astype(F32)).astype(BF16)
-        return carry
-
-    lax.fori_loop(0, keep, norm, 0, unroll=7)
 
     def out_copy(i):
         return pltpu.make_async_remote_copy(
@@ -167,7 +183,7 @@
     @pl.loop(0, CHUNKS)
     def _(c):
         chosen = (iota((SLOTS, toks), 0) + c * SLOTS == key).astype(BF16)
-        put(sent, c * CHUNK, jnp.dot(chosen, hb[...], preferred_element_type=F32))
+        put(sent, c * CHUNK, jnp.dot(chosen, picked[...], preferred_element_type=F32))
 
         @pl.when(c == 0)
         def _():
@@ -175,6 +191,9 @@
             got[0] = sent[0]
 
         each(c, lambda i: out_copy(i).start())
+
+    for copy in small[3:]:
+        copy.wait()
 
     total[...] = jnp.zeros_like(total)
     to_own = (place((1, toks), 1) == iota((toks, 1), 0)).astype(BF16)
@@ -230,6 +249,9 @@
     def _(c):
         each(c, lambda i: out_copy(i).wait_recv())
         take(got, c * CHUNK)
+        for g in range(SLOTS // CHUNK):
+            span = slice(g * CHUNK, (g + 1) * CHUNK)
+            rows[span, :] = normed(rows[span, :].astype(F32)).astype(BF16)
         spare = (even, odd)
         enter(0, even)
         for n in range(1, hidden // step):
@@ -263,32 +285,23 @@
     each(c, lambda i: back_copy(i).wait_recv())
     take(back, c * CHUNK)
     wide = width // 2
-    writes = []
     for n in range(2):
         cols = slice(n * wide, (n + 1) * wide)
         part = total[:, cols] + jnp.dot(sel[c], rows[:, cols], preferred_element_type=F32)
-        hb[:, cols] = (ordered[:, cols].astype(F32) + gate[:, :1] * part).astype(BF16)
-        writes.append(pltpu.make_async_copy(hb.at[:, cols], out.at[:, cols], load_sem.at[n]))
-        writes[-1].start()
+        out[:, cols] = (ordered[:, cols].astype(F32) + gate[:, :1] * part).astype(BF16)
 
     @pl.loop(1, PARTNERS)
     def _(i):
         back_copy(i).wait_send()
 
-    for write in writes:
-        write.wait()
-
-
-def finish_kernel(src, out, buf, in_sem, out_sem):
-    rows = src.shape[0]
-    size = rows // in_sem.shape[0]
-    pieces = [pl.ds(n * size, size) for n in range(in_sem.shape[0])]
-    loads = [pltpu.make_async_copy(src.at[p], buf.at[p], in_sem.at[n]) for n, p in enumerate(pieces)]
-    stores = [pltpu.make_async_copy(buf.at[p], out.at[p], out_sem.at[n]) for n, p in enumerate(pieces)]
-    for copy in loads:
-        copy.start()
-    for n, copy in enumerate(stores):
-        loads[n].wait()
+
+def finish_kernel(src, out, sem):
+    size = src.shape[0] // sem.shape[0]
+    stores = [
+        pltpu.make_async_copy(src.at[pl.ds(n * size, size)], out.at[pl.ds(n * size, size)], sem.at[n])
+        for n in range(sem.shape[0])
+    ]
+    for copy in stores:
         copy.start()
     for copy in stores:
         copy.wait()
@@ -303,18 +316,26 @@
     hidden = w_in.shape[2]
     by_patch = jnp.transpose(patches, (1, 0, 2))
     vmem = pl.BlockSpec(memory_space=pltpu.VMEM)
-    smem = pl.BlockSpec(memory_space=pltpu.SMEM)
     any_ = pl.BlockSpec(memory_space=pl.ANY)
     blk = (experts, 8, 2 * width + 3 * LANES)
     dma = pltpu.SemaphoreType.DMA
     done = jax.ShapeDtypeStruct((toks, width), BF16)
     result = pl.pallas_call(
         layer_kernel,
-        out_shape=done,
-        in_specs=[any_, smem] + [vmem] * 5 + [any_, vmem, any_, vmem],
-        out_specs=any_,
+        out_shape=pltpu.VMEM((toks, width), BF16),
+        in_specs=[any_] * 11,
+        out_specs=vmem,
         scratch_shapes=[
-            pltpu.VMEM(by_patch.shape, BF16),
+            pltpu.VMEM(by_patch.shape[:2] + (width // 2,), BF16),
+            pltpu.VMEM(by_patch.shape[:2] + (width // 2,), BF16),
+            pltpu.SMEM(visible.shape, jnp.int32),
+            pltpu.VMEM((1, toks), jnp.int32),
+            pltpu.VMEM((1, experts), jnp.int32),
+            pltpu.VMEM((1, width), F32),
+            pltpu.VMEM((1, width), F32),
+            pltpu.VMEM((experts, width), F32),
+            pltpu.VMEM((1, hidden), F32),
+            pltpu.VMEM((1, width), F32),
             pltpu.VMEM(blk, BF16),
             pltpu.VMEM(blk, BF16),
             pltpu.VMEM(blk, BF16),
@@ -328,31 +349,31 @@
             pltpu.VMEM((3, 8 * CHUNK, LANES), F32),
             pltpu.VMEM((toks, width), BF16),
             pltpu.VMEM((toks, width), BF16),
-            pltpu.VMEM((toks, width), BF16),
             pltpu.VMEM((toks, LANES), F32),
             pltpu.VMEM((CHUNKS, toks, SLOTS), BF16),
             pltpu.VMEM((toks, width), F32),
-            dma((3,)),
+            dma((12,)),
             dma((experts,)),
             dma((experts,)),
             dma((experts,)),
             dma((experts,)),
         ],
         compiler_params=pltpu.CompilerParams(
-            collective_id=0, has_side_effects=True, vmem_limit_bytes=63 * 2**20
+            collective_id=0, has_side_effects=True, vmem_limit_bytes=58 * 2**20
         ),
         name="layer",
     )(
         by_patch, visible, routes.reshape(1, toks), expert_cap.reshape(1, experts),
         norm_gain.reshape(1, width), norm_bias.reshape(1, width), router.T, w_in, b_in, w_out, b_out,
     )
-    pieces = 7
+    pieces = 2
     return pl.pallas_call(
         finish_kernel,
         out_shape=done,
-        in_specs=[any_],
+        in_specs=[vmem],
         out_specs=any_,
-        scratch_shapes=[pltpu.VMEM((toks, width), BF16), dma((pieces,)), dma((pieces,))],
+        scratch_shapes=[dma((pieces,))],
+        compiler_params=pltpu.CompilerParams(vmem_limit_bytes=4 * 2**20),
         name="finish",
     )(result)
 

time: 78.9 us -> 74.7 us (0.947)
  Pallas kernels: 77.7 us -> 73.3 us
    pallas_call x2, Pallas kernels: 77.7 us -> 73.3 us  [the longest x1 72.1 us: per_device(): pl.pallas_call(layer_kernel, out_shape=pltpu.VMEM((toks, width), BF16), i...]
where the time goes in v4:
time: 74.7 us; the launch traced here: 73.4 us
  Pallas kernels  73.3 us (98%)
    pallas_call x1, Pallas kernels, per_device(): pl.pallas_call(layer_kernel, out_shape=pltpu.VMEM((toks, width), BF16), i...  72.1 us

profile of v4, /device:TPU:0, one launch (start us, length us, event | category | flops | bytes accessed | tf_op | source)
XLA Modules:
  0.0 73.4 jit_solution(5959307825024787799)
XLA Ops:
  0.0 72.1 %layer.1.src = bf16[784,1024]{1,0:T(8,128)(2,1)S(1)} custom-call(bf16[196,16,1024]{2,1,0:T(8,128)(2,1)} %bitcast.6, s32[16,49]{1,0:T(8,128)} %visible_in.1, s32[1,784]{1,0:T(1,128)} %bitcast.10, s32[1,64]{1,0:T(1,128)} %bitcast.11, f32[1,1024]{1,0:T(1,128)} %bitcast.8, f32[1,1024]{1,0:T(1,128)} %bitcast.9, f32[64,1024]{1,0:T(8,128)} %bitcast.7, ...), custom_call_target="tpu_custom_call" | custom-call | tf_op jit(solution)/shard_map/layer/pallas_call | solution.py:323
  72.1 1.2 %finish.1 = bf16[784,1024]{1,0:T(8,128)(2,1)} custom-call(bf16[784,1024]{1,0:T(8,128)(2,1)S(1)} %layer.1.src), custom_call_target="tpu_custom_call" | custom-call | tf_op jit(solution)/shard_map/finish/pallas_call | solution.py:370

commit v5 on v4

--- a/solution.py
+++ b/solution.py
@@ -9,8 +9,8 @@
 SIDE = 4
 LANES = 128
 PARTNERS = SIDE**3
-TURN = 37
-BACKTURN = 45
+TURN = 25
+BACKTURN = 41
 CHUNK = 16
 HIGH = 16 * CHUNK
 SLOTS = 19 * CHUNK

time: 74.7 us -> 73.8 us (0.988); the launches traced: 73.4 us -> 73.7 us
  no operation moved by 1% of the time
where the time goes in v5:
time: 73.8 us; the launch traced here: 73.7 us
  Pallas kernels  73.5 us (100%)
    pallas_call x1, Pallas kernels, per_device(): pl.pallas_call(layer_kernel, out_shape=pltpu.VMEM((toks, width), BF16), i...  72.4 us

profile of v5, /device:TPU:0, one launch (start us, length us, event | category | flops | bytes accessed | tf_op | source)
XLA Modules:
  0.0 73.7 jit_solution(2534514506007814553)
XLA Ops:
  0.0 72.4 %layer.1.src = bf16[784,1024]{1,0:T(8,128)(2,1)S(1)} custom-call(bf16[196,16,1024]{2,1,0:T(8,128)(2,1)} %bitcast.6, s32[16,49]{1,0:T(8,128)} %visible_in.1, s32[1,784]{1,0:T(1,128)} %bitcast.10, s32[1,64]{1,0:T(1,128)} %bitcast.11, f32[1,1024]{1,0:T(1,128)} %bitcast.8, f32[1,1024]{1,0:T(1,128)} %bitcast.9, f32[64,1024]{1,0:T(8,128)} %bitcast.7, ...), custom_call_target="tpu_custom_call" | custom-call | tf_op jit(solution)/shard_map/layer/pallas_call | solution.py:323
  72.4 1.2 %finish.1 = bf16[784,1024]{1,0:T(8,128)(2,1)} custom-call(bf16[784,1024]{1,0:T(8,128)(2,1)S(1)} %layer.1.src), custom_call_target="tpu_custom_call" | custom-call | tf_op jit(solution)/shard_map/finish/pallas_call | solution.py:370

commit v6 on v5

--- a/solution.py
+++ b/solution.py
@@ -9,8 +9,8 @@
 SIDE = 4
 LANES = 128
 PARTNERS = SIDE**3
-TURN = 25
-BACKTURN = 41
+TURN = 41
+BACKTURN = 25
 CHUNK = 16
 HIGH = 16 * CHUNK
 SLOTS = 19 * CHUNK

time: 73.8 us -> 73.7 us (level)
  no operation moved by 1% of the time
where the time goes in v6:
time: 73.7 us; the launch traced here: 73.6 us
  Pallas kernels  73.4 us (100%)
    pallas_call x1, Pallas kernels, per_device(): pl.pallas_call(layer_kernel, out_shape=pltpu.VMEM((toks, width), BF16), i...  72.2 us

profile of v6, /device:TPU:0, one launch (start us, length us, event | category | flops | bytes accessed | tf_op | source)
XLA Modules:
  0.0 73.6 jit_solution(8611116347459223881)
XLA Ops:
  0.0 72.2 %layer.1.src = bf16[784,1024]{1,0:T(8,128)(2,1)S(1)} custom-call(bf16[196,16,1024]{2,1,0:T(8,128)(2,1)} %bitcast.6, s32[16,49]{1,0:T(8,128)} %visible_in.1, s32[1,784]{1,0:T(1,128)} %bitcast.10, s32[1,64]{1,0:T(1,128)} %bitcast.11, f32[1,1024]{1,0:T(1,128)} %bitcast.8, f32[1,1024]{1,0:T(1,128)} %bitcast.9, f32[64,1024]{1,0:T(8,128)} %bitcast.7, ...), custom_call_target="tpu_custom_call" | custom-call | tf_op jit(solution)/shard_map/layer/pallas_call | solution.py:323
  72.2 1.2 %finish.1 = bf16[784,1024]{1,0:T(8,128)(2,1)} custom-call(bf16[784,1024]{1,0:T(8,128)(2,1)S(1)} %layer.1.src), custom_call_target="tpu_custom_call" | custom-call | tf_op jit(solution)/shard_map/finish/pallas_call | solution.py:370
